TPU v7x, 32 devices: a whole 2x2x4 slice. The times are simulated.
32 devices in a mesh: node: 8 (over y, x, core), grp: 4 (over z).
Axes of the slice: x: 2, y: 2, z: 4, core: 2. Of those that a mesh axis runs over, the one named last changes fastest.
Arguments:
- tokens: bfloat16 [12288, 1792], P(('node', 'grp')), may hold values from -6 to 6
- cotangent: bfloat16 [12288, 1792], P(('node', 'grp')), may hold values from -6 to 6
- gate_weight: bfloat16 [1792, 1024], P('node'), may hold values from -0.125 to 0.125
- up_weight: bfloat16 [1792, 1024], P('node'), may hold values from -0.125 to 0.125
- down_weight_t: bfloat16 [1792, 1024], P('node'), may hold values from -0.125 to 0.125
- error_memory: bfloat16 [4, 1792, 3072], P('grp', 'node'), may hold values from -4 to 4
- q_init: float32 [3, 1024, 32], replicated, may hold values from -6 to 6
Outputs:
- token_grad: bfloat16 [12288, 1792], P(('node', 'grp'))
- new_error: bfloat16 [4, 1792, 3072], P('grp', 'node')
- p_hat: float32 [3, 1792, 32], P(None, 'node')
- q_new: float32 [3, 1024, 32], replicated
All inputs are finite; a program needn't handle non-finite values.
Results may differ from a plain program's by a relative error of at most 0.012.
Values may be sent and summed in bfloat16 or wider, within the bound.
A program may use at most 192 MiB of HBM per device.

v0:
```python
import math
import jax
import jax.numpy as jnp
from jax import lax
from jax.sharding import PartitionSpec as P


def gelu_parts(value):
    coeff = math.sqrt(2.0 / math.pi)
    inner = coeff * (value + 0.044715 * value * value * value)
    tanh_value = jnp.tanh(inner)
    activation = 0.5 * value * (1.0 + tanh_value)
    slope = 0.5 * (1.0 + tanh_value) + 0.5 * value * (1.0 - tanh_value * tanh_value) * coeff * (
        1.0 + 3.0 * 0.044715 * value * value
    )
    return (activation, slope)


def contract_rows(left_side, right_side):
    return lax.dot_general(
        left_side, right_side, (((0,), (0,)), ((), ())), preferred_element_type=jnp.float32
    )


def on_device(tokens, cotangent, gate_weight, up_weight, down_weight_t, error_memory, q_init):
    node_count = lax.axis_size("node")
    group_count = lax.axis_size("grp")
    hidden_units = gate_weight.shape[1]
    highest = lax.Precision.HIGHEST
    full_gate, full_up, full_down = (
        lax.all_gather(gate_weight, "node", axis=0, tiled=True),
        lax.all_gather(up_weight, "node", axis=0, tiled=True),
        lax.all_gather(down_weight_t, "node", axis=0, tiled=True),
    )
    gate_pre = jnp.dot(tokens, full_gate, preferred_element_type=jnp.float32)
    up_pre = jnp.dot(tokens, full_up, preferred_element_type=jnp.float32)
    activation, slope = gelu_parts(gate_pre)
    hidden = (activation * up_pre).astype(jnp.bfloat16)
    back_hidden = jnp.dot(cotangent, full_down, preferred_element_type=jnp.float32)
    grad_up = (back_hidden * activation).astype(jnp.bfloat16)
    grad_gate = (back_hidden * up_pre * slope).astype(jnp.bfloat16)
    token_grad = (
        lax.dot_general(
            grad_gate, full_gate, (((1,), (1,)), ((), ())), preferred_element_type=jnp.float32
        )
        + lax.dot_general(
            grad_up, full_up, (((1,), (1,)), ((), ())), preferred_element_type=jnp.float32
        )
    ).astype(jnp.bfloat16)
    gate_up = jnp.concatenate([grad_gate, grad_up], axis=1)
    token_cols, cot_cols = (
        lax.all_to_all(tokens, "node", split_axis=1, concat_axis=0, tiled=True),
        lax.all_to_all(cotangent, "node", split_axis=1, concat_axis=0, tiled=True),
    )
    piece_gu = lax.all_gather(gate_up, "node", axis=0, tiled=True)
    piece_hidden = lax.all_gather(hidden, "node", axis=0, tiled=True)
    summed = jnp.concatenate(
        [contract_rows(token_cols, piece_gu), contract_rows(cot_cols, piece_hidden)], axis=1
    )
    grad_scale = 1.0 / math.sqrt(tokens.shape[0] * node_count)
    merged = summed * grad_scale + error_memory[0].astype(jnp.float32)
    blocks = [merged[:, m * hidden_units : (m + 1) * hidden_units] for m in range(3)]
    row_terms = jnp.stack([jnp.dot(blocks[m], q_init[m], precision=highest) for m in range(3)])
    power_rows = lax.psum(row_terms.astype(jnp.bfloat16), "grp").astype(jnp.float32) / group_count
    local_gram = jnp.einsum("mdr,mds->mrs", power_rows, power_rows, precision=highest)
    gram_matrix = lax.psum(local_gram, "node")
    hats = []
    for m in range(3):
        factor = jnp.linalg.cholesky(gram_matrix[m])
        hats.append(jax.scipy.linalg.solve_triangular(factor, power_rows[m].T, lower=True).T)
    col_terms = jnp.stack([jnp.dot(blocks[m].T, hats[m], precision=highest) for m in range(3)])
    q_new = lax.psum(col_terms, ("node", "grp")) / group_count
    errors = [blocks[m] - jnp.dot(hats[m], q_new[m].T, precision=highest) for m in range(3)]
    new_error = jnp.concatenate(errors, axis=1).astype(jnp.bfloat16)[None]
    return (token_grad, new_error, jnp.stack(hats), q_new)


def solution(mesh):
    return jax.shard_map(
        on_device,
        mesh=mesh,
        in_specs=(
            P(("node", "grp"), None),
            P(("node", "grp"), None),
            P("node", None),
            P("node", None),
            P("node", None),
            P("grp", "node", None),
            P(),
        ),
        out_specs=(P(("node", "grp"), None), P("grp", "node", None), P(None, "node", None), P()),
        check_vma=False,
    )
```

profile of v0, /device:TPU:0, one launch (start us, length us, event | category | flops | bytes accessed | tf_op | source)
XLA Modules:
  0.0 512.1 jit_solution(15546751805123783097)
XLA Ops:
  9.4 37.6 %all-gather.6.cloned.1.call-done = bf16[1792,1024]{1,0:T(8,128)(2,1)} async-done(((bf16[224,1024]{1,0:T(8,128)(2,1)}), bf16[1792,1024]{1,0:T(8,128)(2,1)}) %all-gather.6.cloned.1.call-update) | async-done | bytes 3670032 | tf_op jit(solution)/shard_map/all_gather | solution.py:33
  47.0 5.2 %fusion.44 = f32[384,1024]{1,0:T(8,128)} fusion(bf16[384,1792]{1,0:T(8,128)(2,1)} %param.11, bf16[1792,1024]{1,0:T(8,128)(2,1)} %all-gather.6.cloned.1.call-done), kind=kOutput, calls=%fused_computation.92 | convolution fusion | flops 1409286144 | bytes 6619136 | tf_op jit(solution)/shard_map/dot_general | solution.py:39
  52.2 31.1 %all-gather.10.cloned.1.call-done = bf16[1792,1024]{1,0:T(8,128)(2,1)} async-done(((bf16[224,1024]{1,0:T(8,128)(2,1)}), bf16[1792,1024]{1,0:T(8,128)(2,1)}) %all-gather.10.cloned.1.call-update) | async-done | bytes 3670032 | tf_op jit(solution)/shard_map/all_gather | solution.py:31
  83.3 4.8 fusion.45
  88.1 31.5 %all-gather.8.cloned.1.call-done = bf16[1792,1024]{1,0:T(8,128)(2,1)} async-done(((bf16[224,1024]{1,0:T(8,128)(2,1)}), bf16[1792,1024]{1,0:T(8,128)(2,1)}) %all-gather.8.cloned.1.call-update) | async-done | bytes 3670032 | tf_op jit(solution)/shard_map/all_gather | solution.py:32
  119.6 6.4 %multiply_convert_fusion = (bf16[384,1024]{1,0:T(8,128)(2,1)}, bf16[384,1024]{1,0:T(8,128)(2,1)S(1)}, bf16[384,1024]{1,0:T(8,128)(2,1)S(1)}) fusion(f32[384,1024]{1,0:T(8,128)} %fusion.45, f32[384,1024]{1,0:T(8,128)} %fusion.44, bf16[384,1792]{1,0:T(8,128)(2,1)S(1)} %copy-done.2, bf16[1792,1024]{1,0:T(8,128)(2,1)} %all-gather.8.cloned.1.call-done), kind=kOutput, calls=%fused_computation.15 | convolution fusion | flops 1419116544 | bytes 10551296 | tf_op jit(solution)/shard_map/dot_general | solution.py:36
  126.9 1.4 pad_maximum_fusion
  128.3 1.3 copy-done.1
  129.6 1.5 copy.17
  131.1 3.6 all-to-all-start.1
  134.7 1.5 copy.15
  136.3 24.3 %all-to-all-done.1 = bf16[384,8,224]{0,2,1:T(8,128)(2,1)S(1)} async-done(((bf16[384,8,224]{0,2,1:T(8,128)(2,1)}), bf16[384,8,224]{0,2,1:T(8,128)(2,1)S(1)}, u32[]{:S(2)}, u32[]{:S(2)}) %all-to-all-start.1) | async-done | bytes 1376288 | tf_op jit(solution)/shard_map/all_to_all | solution.py:53
  160.5 3.6 all-to-all-start
  164.3 1.3 copy.25
  165.7 31.9 %all-to-all-done = bf16[384,8,224]{0,2,1:T(8,128)(2,1)S(1)} async-done(((bf16[384,8,224]{0,2,1:T(8,128)(2,1)}), bf16[384,8,224]{0,2,1:T(8,128)(2,1)S(1)}, u32[]{:S(2)}, u32[]{:S(2)}) %all-to-all-start) | async-done | bytes 1376288 | tf_op jit(solution)/shard_map/all_to_all | solution.py:52
  197.6 1.3 copy.24
  198.9 5.4 %fusion.46 = f32[384,1792]{1,0:T(8,128)} fusion(bf16[384,1024]{1,0:T(8,128)(2,1)S(1)} %copy-done.8, bf16[1792,1024]{1,0:T(8,128)(2,1)} %all-gather.10.cloned.1.call-done), kind=kOutput, calls=%fused_computation.94 | convolution fusion | flops 1409286144 | bytes 7208960 | tf_op jit(solution)/shard_map/dot_general | solution.py:43
  204.3 5.4 %convolution_bitcast_fusion.1 = f32[224,1024]{1,0:T(8,128)} fusion(bf16[3072,224]{0,1:T(8,128)(2,1)S(1)} %bitcast.133, bf16[3072,1024]{1,0:T(8,128)(2,1)} %all-gather.14.cloned.1.call-done), kind=kOutput, calls=%fused_computation.19 | convolution fusion | flops 1409286144 | bytes 8585216 | tf_op jit(solution)/shard_map/dot_general | solution.py:20
  209.7 64.7 %all-gather.12.cloned.1.call-done = bf16[3072,2048]{1,0:T(8,128)(2,1)} async-done(((bf16[384,2048]{1,0:T(8,128)(2,1)}), bf16[3072,2048]{1,0:T(8,128)(2,1)}) %all-gather.12.cloned.1.call-update) | async-done | bytes 12582928 | tf_op jit(solution)/shard_map/all_gather | solution.py:55
  274.4 6.4 %convolution_bitcast_fusion = f32[224,2048]{1,0:T(8,128)S(1)} fusion(bf16[3072,224]{0,1:T(8,128)(2,1)S(1)} %bitcast.134, bf16[3072,2048]{1,0:T(8,128)(2,1)} %all-gather.12.cloned.1.call-done), kind=kOutput, calls=%fused_computation.4 | convolution fusion | flops 2818572288 | bytes 15794176 | tf_op jit(solution)/shard_map/dot_general | solution.py:20
  285.2 20.5 %psum.21 = bf16[3,224,32]{1,2,0:T(8,128)(2,1)} all-reduce(bf16[3,224,32]{1,2,0:T(8,128)(2,1)} %pad_maximum_fusion.4), channel_id=1, replica_groups=mesh['node'=8,'grp'=4] {'grp'}, use_global_device_ids=true, to_apply=%region_0.0 | all-reduce | flops 21504 | bytes 86016 | tf_op jit(solution)/shard_map/psum | solution.py:64
  305.6 1.7 fusion.33
  307.4 1.4 convert_multiply_fusion
  308.8 24.0 %psum.22 = f32[3,32,32]{1,2,0:T(8,128)} all-reduce(f32[3,32,32]{1,2,0:T(8,128)} %fusion.33), channel_id=1, replica_groups=mesh['node'=8,'grp'=4] {'node'}, use_global_device_ids=true, to_apply=%region_1.0 | all-reduce | flops 3072 | bytes 24576 | tf_op jit(solution)/shard_map/psum | solution.py:66
  332.9 1.4 slice_bitcast_fusion.14
  335.0 1.4 copy.22
  336.4 1.4 copy.21
  337.8 1.4 fusion.39
  339.2 3.6 cholesky.59
  343.5 1.3 fusion.34
  344.8 3.8 custom-call.7
  348.5 3.6 cholesky.70
  352.9 1.3 fusion.35
  354.1 3.2 custom-call.8
  357.3 1.6 fusion.32
  358.9 1.6 fusion.31
  360.5 3.6 cholesky.81
  364.8 1.3 fusion.36
  366.0 3.2 custom-call.9
  369.2 1.0 fusion.30
  370.9 1.4 convolution_bitcast_fusion.3
  373.8 5.7 %fusion = bf16[384,1792]{1,0:T(8,128)(2,1)} fusion(f32[384,1792]{1,0:T(8,128)} %fusion.46, bf16[384,1024]{1,0:T(8,128)(2,1)S(1)} %get-tuple-element.8, bf16[1792,1024]{1,0:T(8,128)(2,1)} %all-gather.8.cloned.1.call-done), kind=kOutput, calls=%fused_computation.1 | convolution fusion | flops 1410662400 | bytes 8585216 | tf_op jit(solution)/shard_map/dot_general | solution.py:46
  380.2 119.2 %all-reduce.2.cloned.1.call-done = f32[3,1024,32]{1,2,0:T(8,128)} async-done(((f32[3,1024,32]{1,2,0:T(8,128)}), f32[3,1024,32]{1,2,0:T(8,128)}) %all-reduce.2.cloned.1.call-update) | async-done | bytes 393232 | tf_op jit(solution)/shard_map/psum | solution.py:72
  499.4 1.0 broadcast_multiply_fusion
  500.4 1.8 fusion.12
  502.2 0.9 fusion.13
  503.1 0.9 fusion.14
  504.1 1.2 pad_maximum_fusion.1
  (62 shorter events, 13.3 us)
Async XLA Ops:
  7.2 39.8 %all-gather.6.cloned.1.call-start = ((), (), s32[]{:S(2)}) async-start(), calls=%async_computation.2 | async-start | bytes 4128768 | tf_op jit(solution)/shard_map/all_gather | solution.py:33
  7.9 75.4 %all-gather.10.cloned.1.call-start = ((), (), s32[]{:S(2)}) async-start(), calls=%async_computation.4 | async-start | bytes 4128768 | tf_op jit(solution)/shard_map/all_gather | solution.py:31
  8.6 111.0 %all-gather.8.cloned.1.call-start = ((), (), s32[]{:S(2)}) async-start(), calls=%async_computation.3 | async-start | bytes 4128768 | tf_op jit(solution)/shard_map/all_gather | solution.py:32
  9.4 73.9 %copy-start.2 = (bf16[384,1792]{1,0:T(8,128)(2,1)S(1)}, bf16[384,1792]{1,0:T(8,128)(2,1)}, u32[]{:S(2)}) copy-start(bf16[384,1792]{1,0:T(8,128)(2,1)} %param.10) | copy-start | bytes 4128772
  9.4 194.9 %all-gather.14.cloned.1.call-start = ((), (), s32[]{:S(2)}) async-start(), calls=%async_computation.6 | async-start | bytes 7077888 | tf_op jit(solution)/shard_map/all_gather | solution.py:56
  126.0 0.9 copy-start.7
  126.0 148.4 %all-gather.12.cloned.1.call-start = ((), (), s32[]{:S(2)}) async-start(), calls=%async_computation.5 | async-start | bytes 14155776 | tf_op jit(solution)/shard_map/all_gather | solution.py:55
  128.2 1.3 copy-start.1
  131.1 29.4 %all-to-all-start.1 = ((bf16[384,8,224]{0,2,1:T(8,128)(2,1)}), bf16[384,8,224]{0,2,1:T(8,128)(2,1)S(1)}, u32[]{:S(2)}, u32[]{:S(2)}) async-start(bf16[384,8,224]{0,2,1:T(8,128)(2,1)} %bitcast.3), calls=%async_computation.1 | async-start | bytes 2752512 | tf_op jit(solution)/shard_map/all_to_all | solution.py:53
  160.5 37.1 %all-to-all-start = ((bf16[384,8,224]{0,2,1:T(8,128)(2,1)}), bf16[384,8,224]{0,2,1:T(8,128)(2,1)S(1)}, u32[]{:S(2)}, u32[]{:S(2)}) async-start(bf16[384,8,224]{0,2,1:T(8,128)(2,1)} %bitcast), calls=%async_computation | async-start | bytes 2752512 | tf_op jit(solution)/shard_map/all_to_all | solution.py:52
  164.1 335.3 %all-reduce.2.cloned.1.call-start = ((), (), s32[]{:S(2)}) async-start(), calls=%async_computation.7 | async-start | bytes 786432 | tf_op jit(solution)/shard_map/psum | solution.py:72
  197.6 1.3 copy-start.8
  198.9 5.4 %copy-start.4 = (bf16[8,28,8,384]{3,2,0,1:T(8,128)(2,1)S(1)}, bf16[8,28,8,384]{3,2,0,1:T(8,128)(2,1)}, u32[]{:S(2)}) copy-start(bf16[8,28,8,384]{3,2,0,1:T(8,128)(2,1)} %copy.25) | copy-start | bytes 4128772
  204.3 70.1 %copy-start.5 = (bf16[8,28,8,384]{3,2,0,1:T(8,128)(2,1)S(1)}, bf16[8,28,8,384]{3,2,0,1:T(8,128)(2,1)}, u32[]{:S(2)}) copy-start(bf16[8,28,8,384]{3,2,0,1:T(8,128)(2,1)} %copy.24) | copy-start | bytes 4128772
  274.4 6.4 %copy-start.3 = (bf16[1,224,3072]{2,1,0:T(8,128)(2,1)S(1)}, bf16[1,224,3072]{2,1,0:T(8,128)(2,1)}, u32[]{:S(2)}) copy-start(bf16[1,224,3072]{2,1,0:T(8,128)(2,1)} %param.15) | copy-start | bytes 4128772
  274.4 6.4 %copy-start.6 = (f32[224,1024]{1,0:T(8,128)S(1)}, f32[224,1024]{1,0:T(8,128)}, u32[]{:S(2)}) copy-start(f32[224,1024]{1,0:T(8,128)} %convolution_bitcast_fusion.1) | copy-start | bytes 2752516
  280.8 1.0 copy-start.16
  369.2 3.1 copy-start.9
  370.2 2.8 copy-start.14
  373.8 5.7 %copy-start.10 = (f32[32,224]{1,0:T(8,128)S(1)}, f32[32,224]{1,0:T(8,128)}, u32[]{:S(2)}) copy-start(f32[32,224]{1,0:T(8,128)} %fusion.32) | copy-start | bytes 86020
  373.8 5.7 %copy-start.12 = (f32[32,224]{1,0:T(8,128)S(1)}, f32[32,224]{1,0:T(8,128)}, u32[]{:S(2)}) copy-start(f32[32,224]{1,0:T(8,128)} %fusion.31) | copy-start | bytes 86020
  373.8 5.7 %copy-start.15 = (f32[32,224]{1,0:T(8,128)S(1)}, f32[32,224]{1,0:T(8,128)}, u32[]{:S(2)}) copy-start(f32[32,224]{1,0:T(8,128)} %copy-done.14) | copy-start | bytes 86020
  379.5 122.7 %copy-start.13 = (f32[32,224]{1,0:T(8,128)S(1)}, f32[32,224]{1,0:T(8,128)}, u32[]{:S(2)}) copy-start(f32[32,224]{1,0:T(8,128)} %fusion.31) | copy-start | bytes 86020
  500.4 3.7 copy-start
  500.4 2.7 copy-start.11
Sparse Core Ops, SparseCore 0:
  9.9 37.0 all-gather.5
  48.9 34.3 all-gather.9
  85.2 34.3 all-gather.7
  126.1 74.4 all-gather.13
  202.4 71.9 all-gather.11
  373.9 125.4 all-reduce.1
where the time goes:
time: 514 us; the launch traced here: 512 us
  waiting for transfers between devices  342 us (67%)
  matrix products  54.2 us (11%)
  blocking collectives  44.5 us (9%)
  other arithmetic  35.7 us (7%)
  between operations  14.4 us (3%)
  local copies, waits for them, and re-layouts  13.4 us (3%)
  starting transfers between devices  7.6 us (1%)
    psum x1, waiting for transfers between devices, on_device(): q_new = lax.psum(col_terms, ('node', 'grp')) / group_count  119 us
    all_gather x1, waiting for transfers between devices, on_device(): piece_gu = lax.all_gather(gate_up, 'node', axis=0, tiled=True)  64.7 us
    all_gather x1, waiting for transfers between devices, on_device(): lax.all_gather(down_weight_t, 'node', axis=0, tiled=True)  37.6 us
    all_to_all x1, waiting for transfers between devices, on_device(): lax.all_to_all(tokens, 'node', split_axis=1, concat_axis=0, tiled=True)  31.9 us
    all_gather x1, waiting for transfers between devices, on_device(): lax.all_gather(up_weight, 'node', axis=0, tiled=True)  31.5 us
    all_gather x1, waiting for transfers between devices, on_device(): lax.all_gather(gate_weight, 'node', axis=0, tiled=True)  31.1 us
    all_to_all x1, waiting for transfers between devices, on_device(): lax.all_to_all(cotangent, 'node', split_axis=1, concat_axis=0, tiled=True)  24.3 us
    psum x1, blocking collectives, on_device(): gram_matrix = lax.psum(local_gram, 'node')  24 us
  transfers between devices with their start and end apart: 8, of which 7 were waited for; matrix products, arithmetic and copies ran while one was open for 7% of the time, Pallas kernels for 0%

commit v1 on v0

--- a/solution.py
+++ b/solution.py
@@ -52,8 +52,15 @@
         lax.all_to_all(tokens, "node", split_axis=1, concat_axis=0, tiled=True),
         lax.all_to_all(cotangent, "node", split_axis=1, concat_axis=0, tiled=True),
     )
-    piece_gu = lax.all_gather(gate_up, "node", axis=0, tiled=True)
-    piece_hidden = lax.all_gather(hidden, "node", axis=0, tiled=True)
+
+    def handle_seats_all(vector, arr):
+        return jnp.split(
+            jax.lax.all_gather(jnp.concatenate([arr, vector], axis=1), "node", axis=0, tiled=True),
+            [arr.shape[1]],
+            axis=1,
+        )
+
+    piece_gu, piece_hidden = handle_seats_all(hidden, gate_up)
     summed = jnp.concatenate(
         [contract_rows(token_cols, piece_gu), contract_rows(cot_cols, piece_hidden)], axis=1
     )

time: 514 us -> 495 us (0.963)
  waiting for transfers between devices: 342 us -> 325 us
    all_gather x2 -> x1, waiting for transfers between devices: 64.7 us -> 51.8 us  [handle_seats_all(): jax.lax.all_gather(jnp.concatenate([arr, vector], axis=1), 'node', axis=0...]
    all_to_all x1, waiting for transfers between devices: 31.9 us -> 23.5 us  [on_device(): lax.all_to_all(tokens, 'node', split_axis=1, concat_axis=0, tiled=True)]
    all_gather x1, waiting for transfers between devices: 31.1 us -> 37.6 us  [on_device(): lax.all_gather(gate_weight, 'node', axis=0, tiled=True)]
    all_gather x1, waiting for transfers between devices: 37.6 us -> 31.1 us  [on_device(): lax.all_gather(down_weight_t, 'node', axis=0, tiled=True)]
  transfers between devices with their start and end apart: 8 -> 7, of which waited for: 7 -> 7; matrix products, arithmetic and copies ran while one was open for 7% -> 6% of each run, Pallas kernels for 0% -> 0%
where the time goes in v1:
time: 495 us; the launch traced here: 494 us
  waiting for transfers between devices  325 us (66%)
  matrix products  51.8 us (10%)
  blocking collectives  44.5 us (9%)
  other arithmetic  36.6 us (7%)
  between operations  14.1 us (3%)
  local copies, waits for them, and re-layouts  14 us (3%)
  starting transfers between devices  7.52 us (2%)
    psum x1, waiting for transfers between devices, on_device(): q_new = lax.psum(col_terms, ('node', 'grp')) / group_count  119 us
    all_gather x1, waiting for transfers between devices, handle_seats_all(): jax.lax.all_gather(jnp.concatenate([arr, vector], axis=1), 'node', axis=0...  51.8 us
    all_gather x1, waiting for transfers between devices, on_device(): lax.all_gather(gate_weight, 'node', axis=0, tiled=True)  37.6 us
    all_gather x1, waiting for transfers between devices, on_device(): lax.all_gather(up_weight, 'node', axis=0, tiled=True)  31.5 us
    all_gather x1, waiting for transfers between devices, on_device(): lax.all_gather(down_weight_t, 'node', axis=0, tiled=True)  31.1 us
    all_to_all x1, waiting for transfers between devices, on_device(): lax.all_to_all(cotangent, 'node', split_axis=1, concat_axis=0, tiled=True)  28.6 us
    psum x1, blocking collectives, on_device(): gram_matrix = lax.psum(local_gram, 'node')  24 us
    all_to_all x1, waiting for transfers between devices, on_device(): lax.all_to_all(tokens, 'node', split_axis=1, concat_axis=0, tiled=True)  23.5 us
  transfers between devices with their start and end apart: 7, of which 7 were waited for; matrix products, arithmetic and copies ran while one was open for 6% of the time, Pallas kernels for 0%

profile of v1, /device:TPU:0, one launch (start us, length us, event | category | flops | bytes accessed | tf_op | source)
XLA Modules:
  0.0 493.6 jit_solution(3378412146468908143)
XLA Ops:
  9.4 37.6 %all-gather.9.cloned.1.call-done = bf16[1792,1024]{1,0:T(8,128)(2,1)} async-done(((bf16[224,1024]{1,0:T(8,128)(2,1)}), bf16[1792,1024]{1,0:T(8,128)(2,1)}) %all-gather.9.cloned.1.call-update) | async-done | bytes 3670032 | tf_op jit(solution)/shard_map/all_gather | solution.py:31
  47.0 5.2 %fusion.55 = f32[384,1024]{1,0:T(8,128)} fusion(bf16[384,1792]{1,0:T(8,128)(2,1)} %param.10, bf16[1792,1024]{1,0:T(8,128)(2,1)} %all-gather.9.cloned.1.call-done), kind=kOutput, calls=%fused_computation.97 | convolution fusion | flops 1409286144 | bytes 6619136 | tf_op jit(solution)/shard_map/dot_general | solution.py:35
  52.2 31.1 %all-gather.5.cloned.1.call-done = bf16[1792,1024]{1,0:T(8,128)(2,1)} async-done(((bf16[224,1024]{1,0:T(8,128)(2,1)}), bf16[1792,1024]{1,0:T(8,128)(2,1)}) %all-gather.5.cloned.1.call-update) | async-done | bytes 3670032 | tf_op jit(solution)/shard_map/all_gather | solution.py:33
  83.3 4.8 fusion.54
  88.1 31.5 %all-gather.7.cloned.1.call-done = bf16[1792,1024]{1,0:T(8,128)(2,1)} async-done(((bf16[224,1024]{1,0:T(8,128)(2,1)}), bf16[1792,1024]{1,0:T(8,128)(2,1)}) %all-gather.7.cloned.1.call-update) | async-done | bytes 3670032 | tf_op jit(solution)/shard_map/all_gather | solution.py:32
  119.6 5.5 %multiply_convert_fusion = (bf16[384,1024]{1,0:T(8,128)(2,1)S(1)}, bf16[384,1024]{1,0:T(8,128)(2,1)S(1)}, bf16[384,1024]{1,0:T(8,128)(2,1)S(1)}) fusion(f32[384,1024]{1,0:T(8,128)} %fusion.55, f32[384,1024]{1,0:T(8,128)} %fusion.54, bf16[384,1792]{1,0:T(8,128)(2,1)S(1)} %copy-done.2, bf16[1792,1024]{1,0:T(8,128)(2,1)} %all-gather.7.cloned.1.call-done), kind=kOutput, calls=%fused_computation.19 | convolution fusion | flops 1419116544 | bytes 10551296 | tf_op jit(solution)/shard_map/dot_general | solution.py:36
  126.0 1.6 pad_maximum_fusion
  127.6 1.5 copy.17
  129.1 3.6 all-to-all-start.1
  132.7 1.5 copy.15
  134.3 28.6 %all-to-all-done.1 = bf16[384,8,224]{0,2,1:T(8,128)(2,1)S(1)} async-done(((bf16[384,8,224]{0,2,1:T(8,128)(2,1)}), bf16[384,8,224]{0,2,1:T(8,128)(2,1)S(1)}, u32[]{:S(2)}, u32[]{:S(2)}) %all-to-all-start.1) | async-done | bytes 1376288 | tf_op jit(solution)/shard_map/all_to_all | solution.py:53
  162.8 3.6 all-to-all-start
  166.7 1.3 copy.25
  168.0 23.5 %all-to-all-done = bf16[384,8,224]{0,2,1:T(8,128)(2,1)S(1)} async-done(((bf16[384,8,224]{0,2,1:T(8,128)(2,1)}), bf16[384,8,224]{0,2,1:T(8,128)(2,1)S(1)}, u32[]{:S(2)}, u32[]{:S(2)}) %all-to-all-start) | async-done | bytes 1376288 | tf_op jit(solution)/shard_map/all_to_all | solution.py:52
  191.5 1.3 copy.24
  192.8 5.5 %fusion.56 = f32[384,1792]{1,0:T(8,128)} fusion(bf16[384,1024]{1,0:T(8,128)(2,1)S(1)} %copy-done.7, bf16[1792,1024]{1,0:T(8,128)(2,1)} %all-gather.9.cloned.1.call-done), kind=kOutput, calls=%fused_computation.98 | convolution fusion | flops 1409286144 | bytes 7208960 | tf_op jit(solution)/shard_map/dot_general | solution.py:43
  198.4 51.8 %all-gather.11.cloned.1.call-done = bf16[3072,3072]{1,0:T(8,128)(2,1)} async-done(((bf16[384,3072]{1,0:T(8,128)(2,1)}), bf16[3072,3072]{1,0:T(8,128)(2,1)}) %all-gather.11.cloned.1.call-update) | async-done | bytes 18874384 | tf_op jit(solution)/shard_map/all_gather | solution.py:58
  250.2 4.5 fusion.16
  254.7 6.3 %fusion.6 = f32[224,2048]{1,0:T(8,128)S(1)} fusion(bf16[3072,224]{0,1:T(8,128)(2,1)S(1)} %bitcast.132, bf16[3072,3072]{1,0:T(8,128)(2,1)} %all-gather.11.cloned.1.call-done), kind=kOutput, calls=%fused_computation.8 | convolution fusion | flops 2818572288 | bytes 15794176 | tf_op jit(solution)/shard_map/dot_general | solution.py:20
  265.4 20.5 %psum.21 = bf16[3,224,32]{1,2,0:T(8,128)(2,1)} all-reduce(bf16[3,224,32]{1,2,0:T(8,128)(2,1)} %pad_maximum_fusion.4), channel_id=1, replica_groups=mesh['node'=8,'grp'=4] {'grp'}, use_global_device_ids=true, to_apply=%region_0.0 | all-reduce | flops 21504 | bytes 86016 | tf_op jit(solution)/shard_map/psum | solution.py:71
  285.8 1.4 convert_multiply_fusion
  287.3 1.7 fusion.43
  289.0 24.0 %psum.22 = f32[3,32,32]{1,2,0:T(8,128)} all-reduce(f32[3,32,32]{1,2,0:T(8,128)} %fusion.43), channel_id=1, replica_groups=mesh['node'=8,'grp'=4] {'node'}, use_global_device_ids=true, to_apply=%region_1.0 | all-reduce | flops 3072 | bytes 24576 | tf_op jit(solution)/shard_map/psum | solution.py:73
  313.1 1.4 slice_bitcast_fusion.14
  315.2 1.4 copy.21
  316.6 1.4 copy.22
  318.0 1.4 fusion.49
  319.4 3.6 cholesky.81
  323.8 1.3 fusion.46
  325.1 3.2 custom-call.9
  328.2 1.0 fusion.40
  329.9 1.3 convolution_bitcast_fusion
  331.2 3.6 cholesky.70
  335.6 1.3 fusion.45
  336.9 3.2 custom-call.8
  340.0 1.0 fusion.41
  341.7 1.3 convolution_bitcast_fusion.1
  343.0 3.6 cholesky.59
  347.4 1.3 fusion.44
  348.7 3.2 custom-call.7
  351.8 1.0 fusion.42
  354.1 1.7 pad_maximum_fusion.2
  355.9 5.7 %fusion.4 = bf16[384,1792]{1,0:T(8,128)(2,1)} fusion(f32[384,1792]{1,0:T(8,128)} %fusion.56, bf16[384,1024]{1,0:T(8,128)(2,1)S(1)} %get-tuple-element.8, bf16[1792,1024]{1,0:T(8,128)(2,1)} %all-gather.7.cloned.1.call-done), kind=kOutput, calls=%fused_computation.5 | convolution fusion | flops 1410662400 | bytes 8585216 | tf_op jit(solution)/shard_map/dot_general | solution.py:46
  362.3 119.0 %all-reduce.2.cloned.1.call-done = f32[3,1024,32]{1,2,0:T(8,128)} async-done(((f32[3,1024,32]{1,2,0:T(8,128)}), f32[3,1024,32]{1,2,0:T(8,128)}) %all-reduce.2.cloned.1.call-update) | async-done | bytes 393232 | tf_op jit(solution)/shard_map/psum | solution.py:79
  481.2 1.0 broadcast_multiply_fusion
  482.3 1.7 fusion.22
  484.9 0.9 fusion.24
  485.9 1.2 pad_maximum_fusion.1
  (59 shorter events, 14.8 us)
Async XLA Ops:
  7.2 39.8 %all-gather.9.cloned.1.call-start = ((), (), s32[]{:S(2)}) async-start(), calls=%async_computation.4 | async-start | bytes 4128768 | tf_op jit(solution)/shard_map/all_gather | solution.py:31
  7.9 75.4 %all-gather.5.cloned.1.call-start = ((), (), s32[]{:S(2)}) async-start(), calls=%async_computation.2 | async-start | bytes 4128768 | tf_op jit(solution)/shard_map/all_gather | solution.py:33
  8.6 111.0 %all-gather.7.cloned.1.call-start = ((), (), s32[]{:S(2)}) async-start(), calls=%async_computation.3 | async-start | bytes 4128768 | tf_op jit(solution)/shard_map/all_gather | solution.py:32
  9.4 73.9 %copy-start.1 = (bf16[384,1792]{1,0:T(8,128)(2,1)S(1)}, bf16[384,1792]{1,0:T(8,128)(2,1)}, u32[]{:S(2)}) copy-start(bf16[384,1792]{1,0:T(8,128)(2,1)} %param.11) | copy-start | bytes 4128772
  9.4 240.8 %all-gather.11.cloned.1.call-start = ((), (), s32[]{:S(2)}) async-start(), calls=%async_computation.5 | async-start | bytes 21233664 | tf_op jit(solution)/shard_map/all_gather | solution.py:58
  52.2 67.4 %copy-start.2 = (bf16[384,1792]{1,0:T(8,128)(2,1)S(1)}, bf16[384,1792]{1,0:T(8,128)(2,1)}, u32[]{:S(2)}) copy-start(bf16[384,1792]{1,0:T(8,128)(2,1)} %param.10) | copy-start | bytes 4128772
  125.1 0.9 copy-start.6
  129.1 33.7 %all-to-all-start.1 = ((bf16[384,8,224]{0,2,1:T(8,128)(2,1)}), bf16[384,8,224]{0,2,1:T(8,128)(2,1)S(1)}, u32[]{:S(2)}, u32[]{:S(2)}) async-start(bf16[384,8,224]{0,2,1:T(8,128)(2,1)} %bitcast.3), calls=%async_computation.1 | async-start | bytes 2752512 | tf_op jit(solution)/shard_map/all_to_all | solution.py:53
  162.8 28.7 %all-to-all-start = ((bf16[384,8,224]{0,2,1:T(8,128)(2,1)}), bf16[384,8,224]{0,2,1:T(8,128)(2,1)S(1)}, u32[]{:S(2)}, u32[]{:S(2)}) async-start(bf16[384,8,224]{0,2,1:T(8,128)(2,1)} %bitcast), calls=%async_computation | async-start | bytes 2752512 | tf_op jit(solution)/shard_map/all_to_all | solution.py:52
  166.4 314.8 %all-reduce.2.cloned.1.call-start = ((), (), s32[]{:S(2)}) async-start(), calls=%async_computation.6 | async-start | bytes 786432 | tf_op jit(solution)/shard_map/psum | solution.py:79
  168.0 24.9 %copy-start.7 = (bf16[384,1024]{1,0:T(8,128)(2,1)S(1)}, bf16[384,1024]{1,0:T(8,128)(2,1)}, u32[]{:S(2)}) copy-start(bf16[384,1024]{1,0:T(8,128)(2,1)} %copy-done.6) | copy-start | bytes 2359300
  192.8 57.3 %copy-start.4 = (bf16[8,28,8,384]{3,2,0,1:T(8,128)(2,1)S(1)}, bf16[8,28,8,384]{3,2,0,1:T(8,128)(2,1)}, u32[]{:S(2)}) copy-start(bf16[8,28,8,384]{3,2,0,1:T(8,128)(2,1)} %copy.25) | copy-start | bytes 4128772
  250.2 4.5 copy-start.5
  254.7 6.4 %copy-start.3 = (bf16[1,224,3072]{2,1,0:T(8,128)(2,1)S(1)}, bf16[1,224,3072]{2,1,0:T(8,128)(2,1)}, u32[]{:S(2)}) copy-start(bf16[1,224,3072]{2,1,0:T(8,128)(2,1)} %param.15) | copy-start | bytes 4128772
  261.0 1.0 copy-start.16
  329.3 0.6 copy-start.8
  341.0 0.6 copy-start.10
  352.8 0.6 copy-start.13
  355.9 5.7 %copy-start.9 = (f32[32,224]{1,0:T(8,128)S(1)}, f32[32,224]{1,0:T(8,128)}, u32[]{:S(2)}) copy-start(f32[32,224]{1,0:T(8,128)} %copy-done.8) | copy-start | bytes 86020
  355.9 5.7 %copy-start.11 = (f32[32,224]{1,0:T(8,128)S(1)}, f32[32,224]{1,0:T(8,128)}, u32[]{:S(2)}) copy-start(f32[32,224]{1,0:T(8,128)} %copy-done.10) | copy-start | bytes 86020
  355.9 5.7 %copy-start.14 = (f32[32,224]{1,0:T(8,128)S(1)}, f32[32,224]{1,0:T(8,128)}, u32[]{:S(2)}) copy-start(f32[32,224]{1,0:T(8,128)} %copy-done.13) | copy-start | bytes 86020
  361.6 122.4 %copy-start.12 = (f32[32,224]{1,0:T(8,128)S(1)}, f32[32,224]{1,0:T(8,128)}, u32[]{:S(2)}) copy-start(f32[32,224]{1,0:T(8,128)} %copy-done.10) | copy-start | bytes 86020
  361.6 123.3 %copy-start.15 = (f32[32,224]{1,0:T(8,128)S(1)}, f32[32,224]{1,0:T(8,128)}, u32[]{:S(2)}) copy-start(f32[32,224]{1,0:T(8,128)} %copy-done.13) | copy-start | bytes 86020
  482.2 4.8 copy-start
Sparse Core Ops, SparseCore 0:
  9.9 37.0 all-gather.8
  48.9 34.3 all-gather.4
  85.2 34.3 all-gather.6
  127.7 122.3 all-gather.10
  356.0 125.1 all-reduce.1
